TPU v7x, 32 devices: a whole 2x2x4 slice. The times are simulated.
32 devices in a mesh: job: 2 (over core), replica: 4 (over z), model: 4 (over y, x).
Axes of the slice: x: 2, y: 2, z: 4, core: 2. Of those that a mesh axis runs over, the one named last changes fastest.
Arguments:
- grad_query: float32 [8, 1024, 1024], P(('job', 'replica'), None, 'model'), parts along dimension 0, may hold values from -0.875 to 0.875
- grad_key: float32 [8, 1024, 1024], P(('job', 'replica'), None, 'model'), parts along dimension 0, may hold values from -0.875 to 0.875
- grad_value: float32 [8, 1024, 1024], P(('job', 'replica'), None, 'model'), parts along dimension 0, may hold values from -0.875 to 0.875
- grad_mixed: float32 [8, 1024, 1024], P(('job', 'replica'), 'model'), parts along dimension 0, may hold values from -0.875 to 0.875
- grad_norm: float32 [8, 1024], P(('job', 'replica')), parts along dimension 0, may hold values from -8 to 8
- weight_query: float32 [2048, 1024], P(('job', 'replica'), 'model'), parts along dimension 0, may hold values from -0.25 to 0.25
- weight_key: float32 [2048, 1024], P(('job', 'replica'), 'model'), parts along dimension 0, may hold values from -0.25 to 0.25
- weight_value: float32 [2048, 1024], P(('job', 'replica'), 'model'), parts along dimension 0, may hold values from -0.25 to 0.25
- weight_mixed: float32 [2048, 1024], P(('job', 'model'), 'replica'), parts along dimension 0, may hold values from -0.25 to 0.25
- weight_norm: float32 [2048], P(('job', 'replica')), parts along dimension 0, may hold values from 0.25 to 1.75
- moment_query: float32 [2048, 1024], P(('job', 'replica'), 'model'), parts along dimension 0, may hold values from -0.1875 to 0.1875
- moment_key: float32 [2048, 1024], P(('job', 'replica'), 'model'), parts along dimension 0, may hold values from -0.1875 to 0.1875
- moment_value: float32 [2048, 1024], P(('job', 'replica'), 'model'), parts along dimension 0, may hold values from -0.1875 to 0.1875
- moment_mixed: float32 [2048, 1024], P(('job', 'model'), 'replica'), parts along dimension 0, may hold values from -0.1875 to 0.1875
- moment_norm: float32 [2048], P(('job', 'replica')), parts along dimension 0, may hold values from -1.75 to 1.75
Outputs:
- copy_query: bfloat16 [2048, 1024], P('job', 'model'), parts along dimension 0
- copy_key: bfloat16 [2048, 1024], P('job', 'model'), parts along dimension 0
- copy_value: bfloat16 [2048, 1024], P('job', 'model'), parts along dimension 0
- copy_mixed: bfloat16 [2048, 1024], P(('job', 'model')), parts along dimension 0
- copy_norm: bfloat16 [2048], P('job'), parts along dimension 0
- new_query: float32 [2048, 1024], P(('job', 'replica'), 'model'), parts along dimension 0
- new_key: float32 [2048, 1024], P(('job', 'replica'), 'model'), parts along dimension 0
- new_value: float32 [2048, 1024], P(('job', 'replica'), 'model'), parts along dimension 0
- new_mixed: float32 [2048, 1024], P(('job', 'model'), 'replica'), parts along dimension 0
- new_norm: float32 [2048], P(('job', 'replica')), parts along dimension 0
- state_new_query: float32 [2048, 1024], P(('job', 'replica'), 'model'), parts along dimension 0
- state_new_key: float32 [2048, 1024], P(('job', 'replica'), 'model'), parts along dimension 0
- state_new_value: float32 [2048, 1024], P(('job', 'replica'), 'model'), parts along dimension 0
- state_new_mixed: float32 [2048, 1024], P(('job', 'model'), 'replica'), parts along dimension 0
- state_new_norm: float32 [2048], P(('job', 'replica')), parts along dimension 0
There are 2 independent parts, one for each index of `job`. A program takes and returns all parts, laid end to end along the dimension named above; each array names one. Nothing has to cross between parts.
All inputs are finite; a program needn't handle non-finite values.
Results may differ from a plain program's by a relative error of at most 0.0004.
Values may be sent and summed in bfloat16 or wider, within the bound.
No kernel may reach another device: no remote copies, remote signals or barrier semaphores. Data moves between devices by JAX's collectives and lax.ppermute only.
A program may use at most 64 MiB of HBM per device.

v0:
```python
import jax
import jax.numpy as jnp
from jax import lax
from jax.sharding import PartitionSpec as P

learn_rate = 0.5
hold_rate = 0.9


def local(
    grad_query,
    grad_key,
    grad_value,
    grad_mixed,
    grad_norm,
    weight_query,
    weight_key,
    weight_value,
    weight_mixed,
    weight_norm,
    moment_query,
    moment_key,
    moment_value,
    moment_mixed,
    moment_norm,
):
    mean_query, mean_key, mean_value, mean_mixed = (
        lax.psum_scatter(grad_query[0], "replica", scatter_dimension=0, tiled=True),
        lax.psum_scatter(grad_key[0], "replica", scatter_dimension=0, tiled=True),
        lax.psum_scatter(grad_value[0], "replica", scatter_dimension=0, tiled=True),
        lax.psum_scatter(grad_mixed[0], "replica", scatter_dimension=1, tiled=True),
    )
    whole_norm = lax.psum(grad_norm[0], "replica")
    place = lax.axis_index("replica")
    mean_norm = lax.dynamic_slice_in_dim(
        whole_norm, place * weight_norm.shape[0], weight_norm.shape[0]
    )
    mean_rate = lax.axis_size("replica") ** (-0.5)
    mean_query = mean_query * mean_rate
    mean_key = mean_key * mean_rate
    mean_value = mean_value * mean_rate
    mean_mixed = mean_mixed * mean_rate
    mean_norm = mean_norm * mean_rate
    (
        own_query,
        own_key,
        own_value,
        own_mixed,
        slope_query_norm,
        slope_key_norm,
        slope_value_norm,
        slope_mixed_norm,
    ) = lax.psum(
        (
            jnp.sum(weight_query * weight_query, axis=1, keepdims=True),
            jnp.sum(weight_key * weight_key, axis=1, keepdims=True),
            jnp.sum(weight_value * weight_value, axis=1, keepdims=True),
            jnp.sum(weight_mixed * weight_mixed, axis=0, keepdims=True),
            jnp.sum(mean_query * mean_query, axis=1, keepdims=True),
            jnp.sum(mean_key * mean_key, axis=1, keepdims=True),
            jnp.sum(mean_value * mean_value, axis=1, keepdims=True),
            jnp.sum(mean_mixed * mean_mixed, axis=0, keepdims=True),
        ),
        "model",
    )
    mean_query = mean_query * (jnp.sqrt(own_query) * lax.rsqrt(slope_query_norm + 1e-06))
    mean_key = mean_key * (jnp.sqrt(own_key) * lax.rsqrt(slope_key_norm + 1e-06))
    mean_value = mean_value * (jnp.sqrt(own_value) * lax.rsqrt(slope_value_norm + 1e-06))
    mean_mixed = mean_mixed * (jnp.sqrt(own_mixed) * lax.rsqrt(slope_mixed_norm + 1e-06))
    state_new_query = hold_rate * moment_query + mean_query
    new_query = weight_query - learn_rate * state_new_query
    state_new_key = hold_rate * moment_key + mean_key
    new_key = weight_key - learn_rate * state_new_key
    state_new_value = hold_rate * moment_value + mean_value
    new_value = weight_value - learn_rate * state_new_value
    state_new_mixed = hold_rate * moment_mixed + mean_mixed
    new_mixed = weight_mixed - learn_rate * state_new_mixed
    state_new_norm = hold_rate * moment_norm + mean_norm
    new_norm = weight_norm - learn_rate * state_new_norm
    copy_query, copy_key, copy_value, copy_mixed, copy_norm = (
        lax.all_gather(new_query.astype(jnp.bfloat16), "replica", axis=0, tiled=True),
        lax.all_gather(new_key.astype(jnp.bfloat16), "replica", axis=0, tiled=True),
        lax.all_gather(new_value.astype(jnp.bfloat16), "replica", axis=0, tiled=True),
        lax.all_gather(new_mixed.astype(jnp.bfloat16), "replica", axis=1, tiled=True),
        lax.all_gather(new_norm.astype(jnp.bfloat16), "replica", axis=0, tiled=True),
    )
    return (
        copy_query,
        copy_key,
        copy_value,
        copy_mixed,
        copy_norm,
        new_query,
        new_key,
        new_value,
        new_mixed,
        new_norm,
        state_new_query,
        state_new_key,
        state_new_value,
        state_new_mixed,
        state_new_norm,
    )


def solution(mesh):
    placed = (
        P(("job", "replica"), None, "model"),
        P(("job", "replica"), None, "model"),
        P(("job", "replica"), None, "model"),
        P(("job", "replica"), "model", None),
        P(("job", "replica"), None),
        P(("job", "replica"), "model"),
        P(("job", "replica"), "model"),
        P(("job", "replica"), "model"),
        P(("job", "model"), "replica"),
        P(("job", "replica")),
        P(("job", "replica"), "model"),
        P(("job", "replica"), "model"),
        P(("job", "replica"), "model"),
        P(("job", "model"), "replica"),
        P(("job", "replica")),
    )
    return jax.shard_map(
        local,
        mesh=mesh,
        in_specs=placed,
        out_specs=(
            P("job", "model"),
            P("job", "model"),
            P("job", "model"),
            P(("job", "model"), None),
            P("job"),
            P(("job", "replica"), "model"),
            P(("job", "replica"), "model"),
            P(("job", "replica"), "model"),
            P(("job", "model"), "replica"),
            P(("job", "replica")),
            P(("job", "replica"), "model"),
            P(("job", "replica"), "model"),
            P(("job", "replica"), "model"),
            P(("job", "model"), "replica"),
            P(("job", "replica")),
        ),
        check_vma=False,
    )
```

profile of v0, /device:TPU:0, one launch (start us, length us, event | category | flops | bytes accessed | tf_op | source)
XLA Modules:
  0.0 210.1 jit_solution(8399502176376450542)
XLA Ops:
  10.1 13.5 %psum.71 = f32[1024]{0:T(1024)S(1)} all-reduce(f32[1024]{0:T(1024)S(1)} %bitcast.36), channel_id=1, replica_groups=mesh['job'=2,'replica'=4,'model'=4] {'replica'}, use_global_device_ids=true, to_apply=%region_20.0 | all-reduce | flops 1024 | bytes 8192 | tf_op jit(solution)/shard_map/psum | solution.py:33
  24.3 7.7 %all-gather = bf16[4,1,256]{2,1,0:T(2,128)(2,1)S(1)} all-gather(bf16[1,1,256]{2,1,0:T(2,128)(2,1)S(1)} %reshape.38), channel_id=1, replica_groups=mesh['job'=2,'replica'=4,'model'=4] {'replica'}, dimensions={0}, use_global_device_ids=true | all-gather | bytes 2560 | tf_op jit(solution)/shard_map/all_gather | solution.py:85
  32.8 0.8 copy-done
  33.8 6.6 %reduce-scatter.9.cloned.1.call-done = f32[256,256]{1,0:T(8,128)} async-done(((f32[1024,256]{1,0:T(8,128)}), f32[256,256]{1,0:T(8,128)}) %reduce-scatter.9.cloned.1.call-update) | async-done | bytes 262160 | tf_op jit(solution)/shard_map/reduce_scatter | solution.py:30
  40.4 1.1 multiply_reduce_fusion.2
  41.5 27.1 %reduce-scatter.11.cloned.1.call-done = f32[256,256]{1,0:T(8,128)} async-done(((f32[256,1024]{1,0:T(8,128)}), f32[256,256]{1,0:T(8,128)}) %reduce-scatter.11.cloned.1.call-update) | async-done | bytes 262160 | tf_op jit(solution)/shard_map/reduce_scatter | solution.py:31
  68.6 1.0 multiply_reduce_fusion
  69.6 27.1 %reduce-scatter.5.cloned.1.call-done = f32[256,256]{1,0:T(8,128)} async-done(((f32[1024,256]{1,0:T(8,128)}), f32[256,256]{1,0:T(8,128)}) %reduce-scatter.5.cloned.1.call-update) | async-done | bytes 262160 | tf_op jit(solution)/shard_map/reduce_scatter | solution.py:28
  96.7 1.1 multiply_reduce_fusion.6
  97.7 26.9 %reduce-scatter.7.cloned.1.call-done = f32[256,256]{1,0:T(8,128)} async-done(((f32[1024,256]{1,0:T(8,128)}), f32[256,256]{1,0:T(8,128)}) %reduce-scatter.7.cloned.1.call-update) | async-done | bytes 262160 | tf_op jit(solution)/shard_map/reduce_scatter | solution.py:29
  124.7 1.1 multiply_reduce_fusion.4
  125.8 10.0 %all-reduce = (f32[256,1]{0,1:T(1,128)S(1)}, f32[256,1]{0,1:T(1,128)S(1)}, f32[256,1]{0,1:T(1,128)S(1)}, f32[256,1]{0,1:T(1,128)S(1)}, f32[256,1]{0,1:T(1,128)S(...) all-reduce(f32[256,1]{0,1:T(1,128)S(1)} %bitcast.34, ...), channel_id=1, replica_groups=mesh['job'=2,'replica'=4,'model'=4] {'model'}, use_global_device_ids=true, to_apply=%region_4.0 | all-reduce | flops 2048 | bytes 16384 | tf_op jit(solution)/shard_map/psum | solution.py:53
  135.8 0.9 fusion.3
  136.7 14.8 %all_gather.16 = bf16[1024,256]{1,0:T(8,128)(2,1)S(1)} all-gather(bf16[256,256]{1,0:T(8,128)(2,1)S(1)} %get-tuple-element.32), channel_id=1, replica_groups=mesh['job'=2,'replica'=4,'model'=4] {'replica'}, dimensions={0}, use_global_device_ids=true | all-gather | bytes 655360 | tf_op jit(solution)/shard_map/all_gather | solution.py:82
  151.5 0.9 fusion.2
  152.4 15.3 %all_gather.17 = bf16[1024,256]{1,0:T(8,128)(2,1)S(1)} all-gather(bf16[256,256]{1,0:T(8,128)(2,1)S(1)} %get-tuple-element.29), channel_id=1, replica_groups=mesh['job'=2,'replica'=4,'model'=4] {'replica'}, dimensions={0}, use_global_device_ids=true | all-gather | bytes 655360 | tf_op jit(solution)/shard_map/all_gather | solution.py:83
  167.8 0.8 fusion.1
  168.6 16.1 %all_gather.18 = bf16[256,1024]{1,0:T(8,128)(2,1)S(1)} all-gather(bf16[256,256]{1,0:T(8,128)(2,1)S(1)} %get-tuple-element.26), channel_id=1, replica_groups=mesh['job'=2,'replica'=4,'model'=4] {'replica'}, dimensions={1}, use_global_device_ids=true | all-gather | bytes 655360 | tf_op jit(solution)/shard_map/all_gather | solution.py:84
  184.7 0.9 fusion.4
  185.7 14.8 %all_gather.15 = bf16[1024,256]{1,0:T(8,128)(2,1)S(1)} all-gather(bf16[256,256]{1,0:T(8,128)(2,1)S(1)} %get-tuple-element.35), channel_id=1, replica_groups=mesh['job'=2,'replica'=4,'model'=4] {'replica'}, dimensions={0}, use_global_device_ids=true | all-gather | bytes 655360 | tf_op jit(solution)/shard_map/all_gather | solution.py:81
  200.4 0.8 copy.35
  201.2 0.8 copy.36
  202.0 0.8 copy.37
  202.8 0.8 copy.38
  (48 shorter events, 4.6 us)
Async XLA Ops:
  7.2 33.2 %reduce-scatter.9.cloned.1.call-start = ((), (), s32[]{:S(2)}) async-start(), calls=%async_computation.6 | async-start | bytes 1310720 | tf_op jit(solution)/shard_map/reduce_scatter | solution.py:30
  7.9 60.6 %reduce-scatter.11.cloned.1.call-start = ((), (), s32[]{:S(2)}) async-start(), calls=%async_computation.7 | async-start | bytes 1310720 | tf_op jit(solution)/shard_map/reduce_scatter | solution.py:31
  8.7 88.0 %reduce-scatter.5.cloned.1.call-start = ((), (), s32[]{:S(2)}) async-start(), calls=%async_computation.4 | async-start | bytes 1310720 | tf_op jit(solution)/shard_map/reduce_scatter | solution.py:28
  9.4 115.2 %reduce-scatter.7.cloned.1.call-start = ((), (), s32[]{:S(2)}) async-start(), calls=%async_computation.5 | async-start | bytes 1310720 | tf_op jit(solution)/shard_map/reduce_scatter | solution.py:29
  9.4 0.7 copy-start.12
  9.5 14.1 %copy-start.13 = (f32[256]{0:T(256)S(1)}, f32[256]{0:T(256)}, u32[]{:S(2)}) copy-start(f32[256]{0:T(256)} %param.24) | copy-start | bytes 3076
  9.5 14.1 %copy-start.14 = (f32[256]{0:T(256)S(1)}, f32[256]{0:T(256)}, u32[]{:S(2)}) copy-start(f32[256]{0:T(256)} %param.29) | copy-start | bytes 3076
  9.5 23.1 %copy-start.3 = (f32[256,256]{1,0:T(8,128)S(1)}, f32[256,256]{1,0:T(8,128)}, u32[]{:S(2)}) copy-start(f32[256,256]{1,0:T(8,128)} %param.20) | copy-start | bytes 786436
  10.0 22.7 %copy-start.2 = (f32[256,256]{1,0:T(8,128)S(1)}, f32[256,256]{1,0:T(8,128)}, u32[]{:S(2)}) copy-start(f32[256,256]{1,0:T(8,128)} %param.23) | copy-start | bytes 786436
  32.6 1.0 copy-start
  32.7 1.0 copy-start.1
  69.6 66.2 %copy-start.8 = (f32[256,256]{1,0:T(8,128)S(1)}, f32[256,256]{1,0:T(8,128)}, u32[]{:S(2)}) copy-start(f32[256,256]{1,0:T(8,128)} %param.26) | copy-start | bytes 786436
  124.7 11.2 %copy-start.7 = (f32[256,256]{1,0:T(8,128)S(1)}, f32[256,256]{1,0:T(8,128)}, u32[]{:S(2)}) copy-start(f32[256,256]{1,0:T(8,128)} %reduce-scatter.7.cloned.1.call-done) | copy-start | bytes 786436
  136.7 14.8 %copy-start.6 = (f32[256,256]{1,0:T(8,128)S(1)}, f32[256,256]{1,0:T(8,128)}, u32[]{:S(2)}) copy-start(f32[256,256]{1,0:T(8,128)} %reduce-scatter.9.cloned.1.call-done) | copy-start | bytes 786436
  136.7 14.8 %copy-start.9 = (f32[256,256]{1,0:T(8,128)S(1)}, f32[256,256]{1,0:T(8,128)}, u32[]{:S(2)}) copy-start(f32[256,256]{1,0:T(8,128)} %param.27) | copy-start | bytes 786436
  152.4 15.3 %copy-start.5 = (f32[256,256]{1,0:T(8,128)S(1)}, f32[256,256]{1,0:T(8,128)}, u32[]{:S(2)}) copy-start(f32[256,256]{1,0:T(8,128)} %reduce-scatter.11.cloned.1.call-done) | copy-start | bytes 786436
  152.4 15.4 %copy-start.10 = (f32[256,256]{1,0:T(8,128)S(1)}, f32[256,256]{1,0:T(8,128)}, u32[]{:S(2)}) copy-start(f32[256,256]{1,0:T(8,128)} %param.28) | copy-start | bytes 786436
  168.6 16.1 %copy-start.4 = (f32[256,256]{1,0:T(8,128)S(1)}, f32[256,256]{1,0:T(8,128)}, u32[]{:S(2)}) copy-start(f32[256,256]{1,0:T(8,128)} %reduce-scatter.5.cloned.1.call-done) | copy-start | bytes 786436
  168.6 16.1 %copy-start.11 = (f32[256,256]{1,0:T(8,128)S(1)}, f32[256,256]{1,0:T(8,128)}, u32[]{:S(2)}) copy-start(f32[256,256]{1,0:T(8,128)} %param.25) | copy-start | bytes 786436
Sparse Core Ops, SparseCore 0:
  10.3 30.1 reduce-scatter.8
  42.7 25.7 reduce-scatter.10
  70.9 25.7 reduce-scatter.4
  98.8 25.7 reduce-scatter.6
where the time goes:
time: 210 us
  blocking collectives  92.1 us (44%)
  waiting for transfers between devices  90.2 us (43%)
  between operations  14 us (7%)
  other arithmetic  8.91 us (4%)
  local copies, waits for them, and re-layouts  4.75 us (2%)
    reduce_scatter x1, waiting for transfers between devices, local(): lax.psum_scatter(grad_query[0], 'replica', scatter_dimension=0, tiled=True)  27.1 us
    reduce_scatter x1, waiting for transfers between devices, local(): lax.psum_scatter(grad_mixed[0], 'replica', scatter_dimension=1, tiled=True)  27.1 us
    reduce_scatter x1, waiting for transfers between devices, local(): lax.psum_scatter(grad_key[0], 'replica', scatter_dimension=0, tiled=True)  26.9 us
    all_gather x1, blocking collectives, local(): lax.all_gather(new_mixed.astype(jnp.bfloat16), 'replica', axis=1, tiled=T...  16.1 us
    all_gather x1, blocking collectives, local(): lax.all_gather(new_value.astype(jnp.bfloat16), 'replica', axis=0, tiled=T...  15.3 us
    all_gather x1, blocking collectives, local(): lax.all_gather(new_key.astype(jnp.bfloat16), 'replica', axis=0, tiled=True)  14.8 us
    all_gather x1, blocking collectives, local(): lax.all_gather(new_query.astype(jnp.bfloat16), 'replica', axis=0, tiled=T...  14.8 us
    psum x1, blocking collectives, local(): whole_norm = lax.psum(grad_norm[0], 'replica')  13.5 us
  transfers between devices with their start and end apart: 4, of which 4 were waited for; matrix products, arithmetic and copies ran while one was open for 2% of the time, Pallas kernels for 0%

commit v1 on v0

--- a/solution.py
+++ b/solution.py
@@ -5,6 +5,11 @@
 
 learn_rate = 0.5
 hold_rate = 0.9
+
+
+def gathered_along(value, name, dim):
+    pieces = lax.all_gather(value, name)
+    return jnp.concatenate(pieces, axis=dim)
 
 
 def local(
@@ -81,7 +86,7 @@
         lax.all_gather(new_query.astype(jnp.bfloat16), "replica", axis=0, tiled=True),
         lax.all_gather(new_key.astype(jnp.bfloat16), "replica", axis=0, tiled=True),
         lax.all_gather(new_value.astype(jnp.bfloat16), "replica", axis=0, tiled=True),
-        lax.all_gather(new_mixed.astype(jnp.bfloat16), "replica", axis=1, tiled=True),
+        gathered_along(new_mixed.astype(jnp.bfloat16), "replica", 1),
         lax.all_gather(new_norm.astype(jnp.bfloat16), "replica", axis=0, tiled=True),
     )
     return (

time: 210 us -> 210 us (level)
    unnamed x36 -> x35, local copies, waits for them, and re-layouts: 4.75 us -> 4.27 us
where the time goes in v1:
time: 210 us
  blocking collectives  91.6 us (44%)
  waiting for transfers between devices  90.2 us (43%)
  between operations  13.9 us (7%)
  other arithmetic  8.91 us (4%)
  local copies, waits for them, and re-layouts  5.13 us (2%)
    reduce_scatter x1, waiting for transfers between devices, local(): lax.psum_scatter(grad_query[0], 'replica', scatter_dimension=0, tiled=True)  27.1 us
    reduce_scatter x1, waiting for transfers between devices, local(): lax.psum_scatter(grad_mixed[0], 'replica', scatter_dimension=1, tiled=True)  27.1 us
    reduce_scatter x1, waiting for transfers between devices, local(): lax.psum_scatter(grad_key[0], 'replica', scatter_dimension=0, tiled=True)  26.9 us
    all_gather x1, blocking collectives, local(): lax.all_gather(new_value.astype(jnp.bfloat16), 'replica', axis=0, tiled=T...  15.5 us
    all_gather x1, blocking collectives, gathered_along(): pieces = lax.all_gather(value, name)  15.3 us
    all_gather x1, blocking collectives, local(): lax.all_gather(new_key.astype(jnp.bfloat16), 'replica', axis=0, tiled=True)  14.8 us
    all_gather x1, blocking collectives, local(): lax.all_gather(new_query.astype(jnp.bfloat16), 'replica', axis=0, tiled=T...  14.8 us
    psum x1, blocking collectives, local(): whole_norm = lax.psum(grad_norm[0], 'replica')  13.5 us
  transfers between devices with their start and end apart: 4, of which 4 were waited for; matrix products, arithmetic and copies ran while one was open for 2% of the time, Pallas kernels for 0%

profile of v1, /device:TPU:0, one launch (start us, length us, event | category | flops | bytes accessed | tf_op | source)
XLA Modules:
  0.0 209.9 jit_solution(17767544554464997413)
XLA Ops:
  10.1 13.5 %psum.71 = f32[1024]{0:T(1024)S(1)} all-reduce(f32[1024]{0:T(1024)S(1)} %bitcast.43), channel_id=1, replica_groups=mesh['job'=2,'replica'=4,'model'=4] {'replica'}, use_global_device_ids=true, to_apply=%region_20.0 | all-reduce | flops 1024 | bytes 8192 | tf_op jit(solution)/shard_map/psum | solution.py:38
  24.3 7.7 %all-gather.1 = bf16[4,1,256]{2,1,0:T(2,128)(2,1)S(1)} all-gather(bf16[1,1,256]{2,1,0:T(2,128)(2,1)S(1)} %reshape.47), channel_id=1, replica_groups=mesh['job'=2,'replica'=4,'model'=4] {'replica'}, dimensions={0}, use_global_device_ids=true | all-gather | bytes 2560 | tf_op jit(solution)/shard_map/all_gather | solution.py:90
  32.8 0.8 copy-done
  33.8 6.6 %reduce-scatter.9.cloned.1.call-done = f32[256,256]{1,0:T(8,128)} async-done(((f32[1024,256]{1,0:T(8,128)}), f32[256,256]{1,0:T(8,128)}) %reduce-scatter.9.cloned.1.call-update) | async-done | bytes 262160 | tf_op jit(solution)/shard_map/reduce_scatter | solution.py:35
  40.4 1.1 multiply_reduce_fusion.2
  41.5 27.1 %reduce-scatter.11.cloned.1.call-done = f32[256,256]{1,0:T(8,128)} async-done(((f32[256,1024]{1,0:T(8,128)}), f32[256,256]{1,0:T(8,128)}) %reduce-scatter.11.cloned.1.call-update) | async-done | bytes 262160 | tf_op jit(solution)/shard_map/reduce_scatter | solution.py:36
  68.6 1.0 multiply_reduce_fusion
  69.6 27.1 %reduce-scatter.5.cloned.1.call-done = f32[256,256]{1,0:T(8,128)} async-done(((f32[1024,256]{1,0:T(8,128)}), f32[256,256]{1,0:T(8,128)}) %reduce-scatter.5.cloned.1.call-update) | async-done | bytes 262160 | tf_op jit(solution)/shard_map/reduce_scatter | solution.py:33
  96.7 1.1 multiply_reduce_fusion.6
  97.7 26.9 %reduce-scatter.7.cloned.1.call-done = f32[256,256]{1,0:T(8,128)} async-done(((f32[1024,256]{1,0:T(8,128)}), f32[256,256]{1,0:T(8,128)}) %reduce-scatter.7.cloned.1.call-update) | async-done | bytes 262160 | tf_op jit(solution)/shard_map/reduce_scatter | solution.py:34
  124.7 1.1 multiply_reduce_fusion.4
  125.8 10.0 %all-reduce = (f32[256,1]{0,1:T(1,128)S(1)}, f32[256,1]{0,1:T(1,128)S(1)}, f32[256,1]{0,1:T(1,128)S(1)}, f32[256,1]{0,1:T(1,128)S(1)}, f32[256,1]{0,1:T(1,128)S(...) all-reduce(f32[256,1]{0,1:T(1,128)S(1)} %bitcast.41, ...), channel_id=1, replica_groups=mesh['job'=2,'replica'=4,'model'=4] {'model'}, use_global_device_ids=true, to_apply=%region_4.0 | all-reduce | flops 2048 | bytes 16384 | tf_op jit(solution)/shard_map/psum | solution.py:58
  135.8 0.9 fusion.3
  136.7 14.8 %all_gather.19 = bf16[1024,256]{1,0:T(8,128)(2,1)S(1)} all-gather(bf16[256,256]{1,0:T(8,128)(2,1)S(1)} %get-tuple-element.32), channel_id=1, replica_groups=mesh['job'=2,'replica'=4,'model'=4] {'replica'}, dimensions={0}, use_global_device_ids=true | all-gather | bytes 655360 | tf_op jit(solution)/shard_map/all_gather | solution.py:87
  151.5 0.9 fusion.2
  152.4 15.5 %all_gather.20 = bf16[1024,256]{1,0:T(8,128)(2,1)S(1)} all-gather(bf16[256,256]{1,0:T(8,128)(2,1)S(1)} %get-tuple-element.29), channel_id=1, replica_groups=mesh['job'=2,'replica'=4,'model'=4] {'replica'}, dimensions={0}, use_global_device_ids=true | all-gather | bytes 655360 | tf_op jit(solution)/shard_map/all_gather | solution.py:88
  168.0 0.8 fusion.1
  168.9 15.3 %all-gather = bf16[1024,256]{1,0:T(8,128)(2,1)S(1)} all-gather(bf16[256,256]{1,0:T(8,128)(2,1)S(1)} %get-tuple-element.26), channel_id=2, replica_groups=mesh['job'=2,'replica'=4,'model'=4] {'replica'}, dimensions={0}, use_global_device_ids=true | all-gather | bytes 655360 | tf_op jit(solution)/shard_map/all_gather | solution.py:11
  184.2 0.9 copy.33
  185.4 0.9 fusion.4
  186.3 14.8 %all_gather.18 = bf16[1024,256]{1,0:T(8,128)(2,1)S(1)} all-gather(bf16[256,256]{1,0:T(8,128)(2,1)S(1)} %get-tuple-element.35), channel_id=1, replica_groups=mesh['job'=2,'replica'=4,'model'=4] {'replica'}, dimensions={0}, use_global_device_ids=true | all-gather | bytes 655360 | tf_op jit(solution)/shard_map/all_gather | solution.py:86
  201.0 0.8 copy.38
  201.8 0.8 copy.39
  202.6 0.8 copy.40
  (48 shorter events, 4.9 us)
Async XLA Ops:
  7.2 33.2 %reduce-scatter.9.cloned.1.call-start = ((), (), s32[]{:S(2)}) async-start(), calls=%async_computation.6 | async-start | bytes 1310720 | tf_op jit(solution)/shard_map/reduce_scatter | solution.py:35
  7.9 60.6 %reduce-scatter.11.cloned.1.call-start = ((), (), s32[]{:S(2)}) async-start(), calls=%async_computation.7 | async-start | bytes 1310720 | tf_op jit(solution)/shard_map/reduce_scatter | solution.py:36
  8.7 88.0 %reduce-scatter.5.cloned.1.call-start = ((), (), s32[]{:S(2)}) async-start(), calls=%async_computation.4 | async-start | bytes 1310720 | tf_op jit(solution)/shard_map/reduce_scatter | solution.py:33
  9.4 115.2 %reduce-scatter.7.cloned.1.call-start = ((), (), s32[]{:S(2)}) async-start(), calls=%async_computation.5 | async-start | bytes 1310720 | tf_op jit(solution)/shard_map/reduce_scatter | solution.py:34
  9.4 0.7 copy-start.12
  9.5 14.1 %copy-start.13 = (f32[256]{0:T(256)S(1)}, f32[256]{0:T(256)}, u32[]{:S(2)}) copy-start(f32[256]{0:T(256)} %param.24) | copy-start | bytes 3076
  9.5 14.1 %copy-start.14 = (f32[256]{0:T(256)S(1)}, f32[256]{0:T(256)}, u32[]{:S(2)}) copy-start(f32[256]{0:T(256)} %param.29) | copy-start | bytes 3076
  9.5 23.1 %copy-start.3 = (f32[256,256]{1,0:T(8,128)S(1)}, f32[256,256]{1,0:T(8,128)}, u32[]{:S(2)}) copy-start(f32[256,256]{1,0:T(8,128)} %param.20) | copy-start | bytes 786436
  10.0 22.7 %copy-start.2 = (f32[256,256]{1,0:T(8,128)S(1)}, f32[256,256]{1,0:T(8,128)}, u32[]{:S(2)}) copy-start(f32[256,256]{1,0:T(8,128)} %param.23) | copy-start | bytes 786436
  32.6 1.0 copy-start
  32.7 1.0 copy-start.1
  69.6 66.2 %copy-start.8 = (f32[256,256]{1,0:T(8,128)S(1)}, f32[256,256]{1,0:T(8,128)}, u32[]{:S(2)}) copy-start(f32[256,256]{1,0:T(8,128)} %param.26) | copy-start | bytes 786436
  124.7 11.2 %copy-start.7 = (f32[256,256]{1,0:T(8,128)S(1)}, f32[256,256]{1,0:T(8,128)}, u32[]{:S(2)}) copy-start(f32[256,256]{1,0:T(8,128)} %reduce-scatter.7.cloned.1.call-done) | copy-start | bytes 786436
  136.7 14.8 %copy-start.6 = (f32[256,256]{1,0:T(8,128)S(1)}, f32[256,256]{1,0:T(8,128)}, u32[]{:S(2)}) copy-start(f32[256,256]{1,0:T(8,128)} %reduce-scatter.9.cloned.1.call-done) | copy-start | bytes 786436
  136.7 14.8 %copy-start.9 = (f32[256,256]{1,0:T(8,128)S(1)}, f32[256,256]{1,0:T(8,128)}, u32[]{:S(2)}) copy-start(f32[256,256]{1,0:T(8,128)} %param.27) | copy-start | bytes 786436
  152.4 15.6 %copy-start.5 = (f32[256,256]{1,0:T(8,128)S(1)}, f32[256,256]{1,0:T(8,128)}, u32[]{:S(2)}) copy-start(f32[256,256]{1,0:T(8,128)} %reduce-scatter.11.cloned.1.call-done) | copy-start | bytes 786436
  152.4 15.6 %copy-start.10 = (f32[256,256]{1,0:T(8,128)S(1)}, f32[256,256]{1,0:T(8,128)}, u32[]{:S(2)}) copy-start(f32[256,256]{1,0:T(8,128)} %param.28) | copy-start | bytes 786436
  184.2 1.0 copy-start.4
  184.2 1.2 copy-start.11
Sparse Core Ops, SparseCore 0:
  10.3 30.1 reduce-scatter.8
  42.7 25.7 reduce-scatter.10
  70.9 25.7 reduce-scatter.4
  98.8 25.7 reduce-scatter.6
